TPU v7x, 256 devices: a whole 4x4x8 slice. The times are simulated.
256 devices in a mesh: docs: 32 (over x, z), topics: 8 (over y, core).
Axes of the slice: x: 4, y: 4, z: 8, core: 2. Of those that a mesh axis runs over, the one named last changes fastest.
Arguments:
- log_beta: bfloat16 [262144, 2048], P('docs', 'topics'), may hold values from -250 to -4
- gamma_init: float32 [512, 2048], P('docs', 'topics'), may hold values from 0.05 to 5
- topic_prior: float32 [2048], P('topics'), may hold values from 0.02 to 0.5
- word_block: int32 [512, 256, 1], P('docs'), may hold values from 0 to 31; in each aligned block of 4096 rows (0 to 4095, 4096 to 8191, ..., all dimensions but the last counted through in order) at most 256 rows name the same one
- word_row: int32 [512, 256], P('docs'), may hold values from 0 to 8191
- counts: int32 [512, 256], P('docs'), may hold values from 0 to 2
Outputs:
- doc_gamma: float32 [512, 2048], P('docs', 'topics')
- sstats: float32 [262144, 2048], P('docs', 'topics')
Inputs may be any that keep to these rules, and one draw needn't show every extreme that they name: `word_block`: among the token slots of one device's 16 documents, at most 256 name the same vocabulary block, and some block is named by exactly 256 of them on some device. `counts`: A count of 0 marks an empty slot.
All inputs are finite; a program needn't handle non-finite values.
Results may differ from a plain program's by a relative error of at most 0.0003.
Values may be sent and summed in bfloat16 or wider, within the bound.
A program may use at most 64 MiB of HBM per device.

v0:
```python
import functools

import jax
import jax.numpy as jnp
from jax import lax
from jax.experimental import pallas as pl
from jax.experimental.pallas import tpu as pltpu
from jax.sharding import PartitionSpec as P

ITERS = 3
LIFT = 30.0
BF, F32, I32 = jnp.bfloat16, jnp.float32, jnp.int32
NN = (((1,), (0,)), ((), ()))
NT = (((1,), (1,)), ((), ()))
TN = (((0,), (0,)), ((), ()))
MESH = pl.DeviceIdType.MESH
CAP = 256


def dot(a, b, dims=NN):
    return lax.dot_general(a, b, dims, preferred_element_type=F32)


def halves(x):
    high = x.astype(BF)
    return high, (x - high.astype(F32)).astype(BF)


def iota(shape, dim):
    return lax.broadcasted_iota(I32, shape, dim)


def grid_of(owners):
    return {32: 8}.get(owners, owners // 2)


def pack(words, block_ref, row_ref, count_ref, out_ref):
    docs, length = row_ref.shape
    owners = out_ref.shape[0]
    earlier = (iota((length, length), 0) < iota((length, length), 1)).astype(BF)

    def step(d, carry):
        total, offset = carry
        owner, row, count = block_ref[d], row_ref[pl.ds(d, 1), :], count_ref[pl.ds(d, 1), :]
        owner = jnp.where(count > 0, owner, -1)
        member = (iota((owners, length), 0) == owner).astype(F32)
        before = dot(member.astype(BF), earlier) + offset
        rank = jnp.sum(member * before, axis=0, keepdims=True).astype(I32)
        place = (iota((CAP, length), 0) == rank).astype(BF)
        values = jnp.concatenate(
            [
                member * (row % 128).astype(F32),
                member * (row // 128).astype(F32),
                member * (count * docs + d).astype(F32),
            ],
            axis=0,
        ).astype(BF)
        total = total + dot(values, place, NT)
        return total, offset + jnp.sum(member, axis=1, keepdims=True)

    together = 4 if docs % 4 == 0 else 1

    def steps(i, carry):
        for u in range(together):
            carry = step(i * together + u, carry)
        return carry

    total, offset = lax.fori_loop(
        0, docs // together, steps, (jnp.zeros((3 * owners, CAP), F32), jnp.zeros((owners, 1), F32))
    )
    row = (total[owners : 2 * owners] * 128 + total[:owners]).astype(I32)
    row = jnp.minimum(jnp.maximum(row, 0), words - 1)
    row = (row // 8) * 16 + row % 8
    rest = total[2 * owners :].astype(I32)
    used = jnp.broadcast_to(offset, (owners, 128)).astype(I32)
    for half in range(2):
        lanes = slice(half * 128, half * 128 + 128)
        out_ref[:, half, :] = row[:, lanes]
        out_ref[:, 2 + half, :] = rest[:, lanes] % docs
        out_ref[:, 4 + half, :] = rest[:, lanes] // docs
        out_ref[:, 6 + half, :] = used


def exp_digamma(g):
    z = g + 6.0
    total = 1.0 / g
    for i in range(1, 6):
        total = total + 1.0 / (g + float(i))
    inverse = 1.0 / z
    square = inverse * inverse
    series = square * (1 / 12 - square * (1 / 120 - square * (1 / 252 - square * (1 / 240))))
    return jnp.exp(jnp.log(z) - 0.5 * inverse - series - total)


def main_kernel(
    nx, nz, groups,
    block_ref, row_ref, count_ref, gamma_ref, prior_ref, beta_hbm,
    gamma_out, theta_out, weight_out, holder_out, row_out, used_out, high_hbm, low_hbm,
    request, req, rows, beta, wide, raw_a, raw_b, high_ref, low_ref, theta, own_theta,
    shifts, scales, masses, counts, holders, weights, parts, xparts, zbase, zparts,
    local_sem, row_sem, rq_send, rq_recv, shift_send, shift_recv, mass_send, mass_recv,
    tz_send, tz_recv, tx_send, tx_recv, sx_send, sx_recv, sz_send, sz_recv,
):
    owners = nx * nz
    docs = gamma_ref.shape[0]
    me, top = lax.axis_index("docs"), lax.axis_index("topics")
    x, z = me // nz, me % nz
    chunks = nz // 2
    raws = (raw_a, raw_b)
    size = 2 * nx

    def at_x(d):
        return (x + d) % nx

    def at_z(d):
        return (z + d) % nz

    def block(i):
        return pl.ds(pl.multiple_of(i * docs, docs), docs)

    def slots(s):
        return pl.ds(pl.multiple_of(s * CAP, CAP), CAP)

    def lines(c):
        return pl.ds(pl.multiple_of(c * size, size), size)

    def remote(src, dst, send, recv, **device):
        return pltpu.make_async_remote_copy(
            src_ref=src, dst_ref=dst, send_sem=send, recv_sem=recv, device_id=device, device_id_type=MESH
        )

    def each(n, body, first=1):
        lax.fori_loop(first, n, lambda i, _: (body(i), 0)[1], 0)

    barrier = pltpu.get_barrier_semaphore()
    each(
        owners,
        lambda d: pl.semaphore_signal(
            barrier, inc=1, device_id={"docs": (me + d) % owners}, device_id_type=MESH
        ),
    )
    for d in range(1, groups):
        pl.semaphore_signal(barrier, inc=1, device_id={"topics": (top + d) % groups}, device_id_type=MESH)
    load = pltpu.make_async_copy(beta_hbm, beta, local_sem.at[0])
    load.start()
    pack(beta.shape[0], block_ref, row_ref, count_ref, request)
    first = exp_digamma(gamma_ref[...])
    own_theta[...] = first
    theta[block(me), :] = first
    req[me] = request[me]
    pl.semaphore_wait(barrier, owners - 1 + groups - 1)

    def turn(k):
        return jnp.where(k % 2 == 1, (k + 1) // 2, (nz - k // 2) % nz)

    def rq_copy(k, d):
        to, q = at_x(d) * nz + at_z(turn(k)), k * nx + d
        return remote(request.at[to], req.at[me], rq_send.at[q], rq_recv.at[q], docs=to)

    def others(action):
        for d in range(1, nx):
            action(0, d)

        def row(k):
            for d in range(nx):
                action(k, d)

        each(nz, row)

    def tz_copy(d):
        return remote(theta.at[block(me)], theta.at[block(me)], tz_send.at[d], tz_recv.at[d], docs=x * nz + at_z(d))

    def tx_copy(dx, dz):
        b = block(x * nz + at_z(nz - dz))
        return remote(theta.at[b], theta.at[b], tx_send.at[dx, dz], tx_recv.at[dx, dz], docs=at_x(dx) * nz + z)

    def sx_copy(dx, dz):
        b = block(at_x(dx) * nz + at_z(dz))
        return remote(parts.at[b], xparts.at[dx, dz], sx_send.at[dx, dz], sx_recv.at[dx, dz], docs=at_x(dx) * nz + z)

    def sz_copy(d):
        return remote(zbase.at[d], zparts.at[d], sz_send.at[d], sz_recv.at[d], docs=x * nz + at_z(d))

    def shift_copy(d, c):
        a = shifts.at[top, lines(c)]
        return remote(a, a, shift_send.at[d, c], shift_recv.at[d, c], topics=(top + d) % groups)

    def mass_copy(p, d, c):
        a = masses.at[p, top, lines(c)]
        return remote(a, a, mass_send.at[d, c], mass_recv.at[p, d, c], topics=(top + d) % groups)

    def source(k, d):
        return at_x(nx - d) * nz + at_z(nz - turn(k))

    def send_theta():
        each(nz, lambda d: tz_copy(d).start())
        for d in range(1, nx):
            tx_copy(d, 0).start()

    def forward(k):
        dz = turn(k)
        tz_copy(dz).wait_recv()
        for d in range(1, nx):
            tx_copy(d, dz).start()

    def forwards(c):
        each(jnp.minimum(2 * c + 4, nz), forward, 2 * c + 2)

    def mass_of(p, k, d):
        s, q = source(k, d), k * nx + d
        high, low = halves(theta[block(s), :])
        both = dot(jnp.concatenate([high, low], axis=0), high_ref[slots(s), :], NT)
        mass = both[:docs] + both[docs:] + dot(high, low_ref[slots(s), :], NT)
        mine = iota((docs, CAP), 0) == holders[pl.ds(q, 1), :]
        masses[p, top, pl.ds(q, 1), :] = jnp.sum(jnp.where(mine, mass, 0.0), axis=0, keepdims=True)

    def masses_of(p, c):
        for k in (2 * c, 2 * c + 1):
            for d in range(1, nx):
                tx_copy(d, turn(k)).wait_recv()
        for k in (2 * c, 2 * c + 1):
            for d in range(nx):
                mass_of(p, k, d)
        each(groups, lambda d: mass_copy(p, d, c).start())

    def sent_theta():
        each(nz, lambda d: tz_copy(d).wait_send())

        def sent(k):
            for d in range(1, nx):
                tx_copy(d, k).wait_send()

        each(nz, sent, 0)

    others(lambda k, d: rq_copy(k, d).start())
    send_theta()
    load.wait()

    def widen(i):
        value = beta[slots(i), :].astype(F32)
        for n in range(0, CAP, 8):
            for half in range(2):
                to = pl.ds(pl.multiple_of(i * 2 * CAP + 2 * n + 8 * half, 8), 8)
                wide[to, :] = value[n : n + 8, half * 128 : half * 128 + 128]

    each(beta.shape[0] // CAP, widen, 0)

    def to_scalars(q):
        s = source(q // nx, q % nx)
        return pltpu.make_async_copy(req.at[s, 0:2, :], rows.at[s], row_sem.at[q])

    def arrive(q):
        @pl.when(q > 0)
        def _():
            rq_copy(q // nx, q % nx).wait_recv()

        to_scalars(q).start()
        s, at = source(q // nx, q % nx), pl.ds(q, 1)
        holders[at, :] = jnp.concatenate([req[s, 2:3, :], req[s, 3:4, :]], axis=1)
        counts[at, :] = jnp.concatenate([req[s, 4:5, :], req[s, 5:6, :]], axis=1).astype(F32)

    each(size, arrive, 0)
    each(2, forward)
    lead = (iota((8, 128), 1) == 0).astype(BF)

    def fetch(i):
        pair = (2 * i, 2 * i + 1)
        homes = [source(q // nx, q % nx) for q in pair]
        for q in pair:
            to_scalars(q).wait()
        for s, raw in zip(homes, raws):
            for start in range(0, CAP, 16):
                values = [
                    wide[pl.ds(rows[s, n // 128, n % 128], 2, stride=8), :] for n in range(start, start + 16)
                ]
                for u in range(16):
                    raw[pl.ds(2 * start + u // 8 * 16 + u % 8, 2, stride=8), :] = values[u]
        for q, s, raw in zip(pair, homes, raws):
            sides = [
                jnp.concatenate([raw[n + 8 * half : n + 8 * half + 8, :] for n in range(0, 2 * CAP, 16)], axis=0)
                for half in range(2)
            ]
            peak = jnp.max(jnp.maximum(*sides), axis=1, keepdims=True)
            for half in range(2):
                high, low = halves(jnp.exp(sides[half] - (peak - LIFT)))
                high_ref[slots(s), half * 128 : half * 128 + 128] = high
                low_ref[slots(s), half * 128 : half * 128 + 128] = low
            peaks = dot(lead, jnp.broadcast_to(peak, (CAP, 128)).astype(BF), NT)
            shifts[top, pl.ds(q, 1), :] = peaks[:1] - LIFT

    def begin(c):
        forwards(c)
        each(jnp.minimum(size * (c + 2), owners), arrive, size * (c + 1))
        each(nx * (c + 1), fetch, nx * c)
        each(groups, lambda d: shift_copy(d, c).start())
        masses_of(0, c)

    each(chunks, begin, 0)
    keeps = [
        pltpu.make_async_copy(high_ref, high_hbm, local_sem.at[0]),
        pltpu.make_async_copy(low_ref, low_hbm, local_sem.at[1]),
    ]
    for copy in keeps:
        copy.start()
    sent_theta()
    others(lambda k, d: rq_copy(k, d).wait_send())

    def scale(c):
        each(groups, lambda d: shift_copy(d, c).wait())
        peak = shifts[0, lines(c), :]
        for t in range(1, groups):
            peak = jnp.maximum(peak, shifts[t, lines(c), :])
        for t in range(groups):
            scales[t, lines(c), :] = jnp.exp(shifts[t, lines(c), :] - peak)

    def weigh(p, c):
        each(groups, lambda d: mass_copy(p, d, c).wait())
        norm = scales[0, lines(c), :] * masses[p, 0, lines(c), :]
        for t in range(1, groups):
            norm = norm + scales[t, lines(c), :] * masses[p, t, lines(c), :]
        weights[lines(c), :] = counts[lines(c), :] * scales[top, lines(c), :] / norm

    def part_of(k, d):
        s, q = source(k, d), k * nx + d
        mine = iota((docs, CAP), 0) == holders[pl.ds(q, 1), :]
        high, low = halves(jnp.where(mine, weights[pl.ds(q, 1), :], 0.0))
        both = dot(jnp.concatenate([high, low], axis=0), high_ref[slots(s), :])
        parts[block(s), :] = both[:docs] + both[docs:] + dot(high, low_ref[slots(s), :])

    def back(k):
        return (nz - turn(k)) % nz

    def parts_of(c):
        for k in (2 * c, 2 * c + 1):
            for d in range(nx):
                part_of(k, d)
        for k in (2 * c, 2 * c + 1):
            for d in range(1, nx):
                sx_copy(d, back(k)).start()

    def joined(dz):
        total = parts[block(x * nz + at_z(dz)), :]
        for d in range(1, nx):
            sx_copy(d, dz).wait_recv()
            total = total + xparts[d, dz]
        return total

    def onward(k):
        zbase[back(k)] = joined(back(k))
        sz_copy(back(k)).start()

    def renew(p, prepare):
        def share(c):
            prepare(c)
            weigh(p, c)
            parts_of(c)

        each(chunks, share, 0)
        each(nz, onward)
        total = joined(0)
        for d in range(1, nz):
            sz_copy(d).wait_recv()
            total = total + zparts[d]
        gamma = prior_ref[...] + own_theta[...] * total
        gamma_out[...] = gamma
        new = exp_digamma(gamma)
        own_theta[...] = new
        theta[block(me), :] = new
        send_theta()
        each(nz, lambda d: sz_copy(d).wait_send())

        def sent(k):
            for d in range(1, nx):
                sx_copy(d, k).wait_send()

        each(nz, sent, 0)

    def collect(p):
        each(2, forward)
        each(
            chunks,
            lambda c: (forwards(c), masses_of(p, c)),
            0,
        )
        sent_theta()

    renew(0, scale)

    def sweep(i):
        collect(i % 2)
        renew(i % 2, lambda c: None)

    each(ITERS, sweep)
    collect(ITERS % 2)
    each(chunks, lambda c: weigh(ITERS % 2, c), 0)

    def deliver(k):
        for d in range(nx):
            s, q = source(k, d), pl.ds(k * nx + d, 1)
            weight_out[pl.ds(s, 1), :] = weights[q, :]
            holder_out[pl.ds(s, 1), :] = holders[q, :]
            used_out[pl.ds(s, 1), :] = req[s, 6:7, :]
            for half in range(2):
                row_out[pl.ds(2 * s + half, 1), :] = req[s, half : half + 1, :]

    each(nz, deliver, 0)
    theta_out[...] = theta[...]
    for copy in keeps:
        copy.wait()


def stats_kernel(
    docs, rows_ref, used_ref, holder_ref, theta_ref, weight_ref, gamma_ref, high_hbm, low_hbm, gamma_out, out_hbm,
    terms, high_ref, low_ref, sem, *sums,
):
    loads = [
        pltpu.make_async_copy(high_hbm, high_ref, sem.at[0]),
        pltpu.make_async_copy(low_hbm, low_ref, sem.at[1]),
    ]
    for copy in loads:
        copy.start()
    gamma_out[...] = gamma_ref[...]
    owners = holder_ref.shape[0]
    lines = out_hbm.shape[0]

    def clear(i, _):
        for total in sums:
            total[pl.ds(pl.multiple_of(i * CAP, CAP), CAP), :] = jnp.zeros((CAP, 128), F32)
        return 0

    lax.fori_loop(0, lines // CAP, clear, 0)
    for copy in loads:
        copy.wait()

    def term(s):
        weight = jnp.where(iota((docs, CAP), 0) == holder_ref[pl.ds(s, 1), :], weight_ref[pl.ds(s, 1), :], 0.0)
        whigh, wlow = halves(weight)
        thigh, tlow = halves(theta_ref[pl.ds(pl.multiple_of(s * docs, docs), docs), :])
        at = pl.ds(pl.multiple_of(s * CAP, CAP), CAP)
        share = dot(
            jnp.concatenate([whigh, whigh, wlow], axis=0), jnp.concatenate([thigh, tlow, thigh], axis=0), TN
        )
        term = share * (high_ref[at, :].astype(F32) + low_ref[at, :].astype(F32))
        for n in range(0, CAP, 8):
            for half in range(2):
                to = pl.ds(pl.multiple_of(s * 2 * CAP + 2 * n + 8 * half, 8), 8)
                terms[to, :] = term[n : n + 8, half * 128 : half * 128 + 128]

    def four(i, _):
        for u in range(4):
            term(i * 4 + u)
        return 0

    lax.fori_loop(0, owners // 4, four, 0)
    group = 16

    def one(s, _):
        def add(j, _):
            base = pl.multiple_of(s * CAP + j * group, group)
            now = terms.at[pl.ds(pl.multiple_of(2 * base, 2 * group), 2 * group), :]
            rows = [rows_ref[base + u] for u in range(group)]
            for start in range(0, group, len(sums)):
                news = []
                for k, total in enumerate(sums):
                    u = start + k
                    news.append(total[pl.ds(rows[u], 2, stride=8), :] + now[pl.ds(u // 8 * 16 + u % 8, 2, stride=8), :])
                for k, total in enumerate(sums):
                    total[pl.ds(rows[start + k], 2, stride=8), :] = news[k]
            return 0

        lax.fori_loop(0, (used_ref[s, 0] + group - 1) // group, add, 0)
        return 0

    lax.fori_loop(0, owners, one, 0)

    def finish(i, _):
        at = pl.ds(pl.multiple_of(i * CAP, CAP), CAP)
        sums[0][at, :] = functools.reduce(jnp.add, [total[at, :] for total in sums])
        pltpu.make_async_copy(sums[0].at[at], out_hbm.at[at], sem.at[2]).start()
        return 0

    lax.fori_loop(0, lines // CAP, finish, 0)
    pltpu.make_async_copy(sums[0], out_hbm, sem.at[2]).wait()


VM = pl.BlockSpec(memory_space=pltpu.VMEM)
SM = pl.BlockSpec(memory_space=pltpu.SMEM)
AN = pl.BlockSpec(memory_space=pl.ANY)


def call(kernel, outs, in_specs, out_specs, scratch, **params):
    return pl.pallas_call(
        kernel,
        out_shape=outs,
        in_specs=in_specs,
        out_specs=out_specs,
        scratch_shapes=list(scratch),
        compiler_params=pltpu.CompilerParams(vmem_limit_bytes=60 * 2**20, **params),
    )


def shape(s, t=F32):
    return jax.ShapeDtypeStruct(s, t)


def per_device(log_beta, gamma_init, topic_prior, word_block, word_row, counts):
    docs, length = counts.shape
    words, cols = log_beta.shape
    owners, groups = lax.axis_size("docs"), lax.axis_size("topics")
    nz = grid_of(owners)
    nx = owners // nz
    slots = owners * CAP
    D, V = pltpu.SemaphoreType.DMA, pltpu.VMEM
    block = (docs, cols)
    gamma, theta, weight, holder, rows, used, high, low = call(
        functools.partial(main_kernel, nx, nz, groups),
        [
            shape(block), shape((owners * docs, cols)), shape((owners, CAP)), shape((owners, CAP), I32),
            shape((2 * owners, 128), I32), shape((owners, 128), I32),
            shape((slots, cols), BF), shape((slots, cols), BF),
        ],
        [VM] * 5 + [AN],
        [VM] * 6 + [AN] * 2,
        [
            V((owners, 8, 128), I32),
            V((owners, 8, 128), I32),
            pltpu.SMEM((owners, 2, 128), I32),
            V((words, cols), BF),
            V((2 * words, 128), F32),
            V((2 * CAP, 128), F32),
            V((2 * CAP, 128), F32),
            V((slots, cols), BF),
            V((slots, cols), BF),
            V((owners * docs, cols), F32),
            V(block, F32),
            V((groups, owners, CAP), F32),
            V((groups, owners, CAP), F32),
            V((2, groups, owners, CAP), F32),
            V((owners, CAP), F32),
            V((owners, CAP), I32),
            V((owners, CAP), F32),
            V((owners * docs, cols), F32),
            V((nx, nz, *block), F32),
            V((nz, *block), F32),
            V((nz, *block), F32),
            D((2,)), D((owners,)), D((owners,)), D((owners,)), D((groups, nz // 2)), D((groups, nz // 2)),
            D((groups, nz // 2)), D((2, groups, nz // 2)),
            D((nz,)), D((nz,)), D((nx, nz)), D((nx, nz)), D((nx, nz)), D((nx, nz)), D((nz,)), D((nz,)),
        ],
        collective_id=1,
        has_side_effects=True,
    )(jnp.swapaxes(word_block, 1, 2), word_row, counts, gamma_init, topic_prior[None, :], log_beta)
    gamma, stats = call(
        functools.partial(stats_kernel, docs),
        [shape(block), shape((2 * words, 128))],
        [SM, SM] + [VM] * 4 + [AN] * 2,
        [VM, AN],
        [V((2 * slots, 128), F32), V((slots, cols), BF), V((slots, cols), BF), D((3,))]
        + [V((2 * words, 128), F32)] * 4,
    )(rows.reshape(slots), used, holder, theta, weight, gamma, high, low)
    return gamma, stats.reshape(words // 8, 2, 8, 128).swapaxes(1, 2).reshape(words, cols)


def solution(mesh):
    return jax.shard_map(
        per_device,
        mesh=mesh,
        in_specs=(
            P("docs", "topics"),
            P("docs", "topics"),
            P("topics"),
            P("docs", None, None),
            P("docs", None),
            P("docs", None),
        ),
        out_specs=(P("docs", "topics"), P("docs", "topics")),
        check_vma=False,
    )
```

profile of v0, /device:TPU:5, one launch (start us, length us, event | category | flops | bytes accessed | tf_op | source)
XLA Modules:
  0.0 147.7 jit_solution(2115130380475010843)
XLA Ops:
  0.6 126.0 %shard_map.77 = (f32[16,256]{1,0:T(8,128)}, f32[512,256]{1,0:T(8,128)}, f32[32,256]{1,0:T(8,128)}, s32[32,256]{1,0:T(8,128)}, s32[64,128]{1,0:T(8,128)}, /*index...) custom-call(s32[16,1,256]{2,1,0:T(1,128)} %bitcast.9, s32[16,256]{1,0:T(8,128)} %row_ref.1, ...), custom_call_target="tpu_custom_call" | custom-call | tf_op jit(solution)/shard_map/pallas_call | solution.py:515
  126.7 21.1 %shard_map.78 = (f32[16,256]{1,0:T(8,128)}, f32[16384,128]{1,0:T(8,128)}) custom-call(s32[8192]{0:T(1024)} %bitcast.8, s32[32,128]{1,0:T(8,128)} %get-tuple-element.13.used_ref, s32[32,256]{1,0:T(8,128)} %get-tuple-element.14.holder_ref, f32[512,256]{1,0:T(8,128)} %get-tuple-element.15.theta_ref, f32[32,256]{1,0:T(8,128)} %get-tuple-element.16.weight_ref, ...), custom_call_target="tpu_custom_call" | custom-call | tf_op jit(solution)/shard_map/pallas_call | solution.py:553
where the time goes:
time: 148 us
  Pallas kernels  147 us (99%)
    pallas_call x1, Pallas kernels, per_device(): call(functools.partial(main_kernel, nx, nz, groups), [shape(block), shape...  126 us
    pallas_call x1, Pallas kernels, per_device(): call(functools.partial(stats_kernel, docs), [shape(block), shape((2 * wor...  21.1 us

commit v1 on v0

--- a/solution.py
+++ b/solution.py
@@ -95,7 +95,7 @@
 def main_kernel(
     nx, nz, groups,
     block_ref, row_ref, count_ref, gamma_ref, prior_ref, beta_hbm,
-    gamma_out, theta_out, weight_out, holder_out, row_out, used_out, high_hbm, low_hbm,
+    gamma_out, theta_hbm, weight_out, holder_out, row_out, used_out, high_hbm, low_hbm,
     request, req, rows, beta, wide, raw_a, raw_b, high_ref, low_ref, theta, own_theta,
     shifts, scales, masses, counts, holders, weights, parts, xparts, zbase, zparts,
     local_sem, row_sem, rq_send, rq_recv, shift_send, shift_recv, mass_send, mass_recv,
@@ -106,6 +106,7 @@
     me, top = lax.axis_index("docs"), lax.axis_index("topics")
     x, z = me // nz, me % nz
     chunks = nz // 2
+    spread = sorted(range(1, nx), key=lambda d: abs(2 * d - nx))
     raws = (raw_a, raw_b)
     size = 2 * nx
 
@@ -193,14 +194,15 @@
         return at_x(nx - d) * nz + at_z(nz - turn(k))
 
     def send_theta():
-        each(nz, lambda d: tz_copy(d).start())
         for d in range(1, nx):
             tx_copy(d, 0).start()
+        for k in range(1, nz):
+            tz_copy((k + 1) // 2 if k % 2 else nz - k // 2).start()
 
     def forward(k):
         dz = turn(k)
         tz_copy(dz).wait_recv()
-        for d in range(1, nx):
+        for d in spread:
             tx_copy(d, dz).start()
 
     def forwards(c):
@@ -221,7 +223,8 @@
         for k in (2 * c, 2 * c + 1):
             for d in range(nx):
                 mass_of(p, k, d)
-        each(groups, lambda d: mass_copy(p, d, c).start())
+        for d in range(1, groups):
+            mass_copy(p, d, c).start()
 
     def sent_theta():
         each(nz, lambda d: tz_copy(d).wait_send())
@@ -314,7 +317,8 @@
             scales[t, lines(c), :] = jnp.exp(shifts[t, lines(c), :] - peak)
 
     def weigh(p, c):
-        each(groups, lambda d: mass_copy(p, d, c).wait())
+        for d in range(1, groups):
+            mass_copy(p, d, c).wait()
         norm = scales[0, lines(c), :] * masses[p, 0, lines(c), :]
         for t in range(1, groups):
             norm = norm + scales[t, lines(c), :] * masses[p, t, lines(c), :]
@@ -335,7 +339,7 @@
             for d in range(nx):
                 part_of(k, d)
         for k in (2 * c, 2 * c + 1):
-            for d in range(1, nx):
+            for d in spread:
                 sx_copy(d, back(k)).start()
 
     def joined(dz):
@@ -376,12 +380,8 @@
         each(nz, sent, 0)
 
     def collect(p):
-        each(2, forward)
-        each(
-            chunks,
-            lambda c: (forwards(c), masses_of(p, c)),
-            0,
-        )
+        each(nz, forward)
+        each(chunks, lambda c: masses_of(p, c), 0)
         sent_theta()
 
     renew(0, scale)
@@ -392,30 +392,37 @@
 
     each(ITERS, sweep)
     collect(ITERS % 2)
-    each(chunks, lambda c: weigh(ITERS % 2, c), 0)
+    keep = pltpu.make_async_copy(theta, theta_hbm, local_sem.at[2])
+    keep.start()
 
     def deliver(k):
         for d in range(nx):
             s, q = source(k, d), pl.ds(k * nx + d, 1)
-            weight_out[pl.ds(s, 1), :] = weights[q, :]
             holder_out[pl.ds(s, 1), :] = holders[q, :]
             used_out[pl.ds(s, 1), :] = req[s, 6:7, :]
             for half in range(2):
                 row_out[pl.ds(2 * s + half, 1), :] = req[s, half : half + 1, :]
 
     each(nz, deliver, 0)
-    theta_out[...] = theta[...]
-    for copy in keeps:
+    each(chunks, lambda c: weigh(ITERS % 2, c), 0)
+
+    def hand_out(k):
+        for d in range(nx):
+            weight_out[pl.ds(source(k, d), 1), :] = weights[pl.ds(k * nx + d, 1), :]
+
+    each(nz, hand_out, 0)
+    for copy in (*keeps, keep):
         copy.wait()
 
 
 def stats_kernel(
-    docs, rows_ref, used_ref, holder_ref, theta_ref, weight_ref, gamma_ref, high_hbm, low_hbm, gamma_out, out_hbm,
-    terms, high_ref, low_ref, sem, *sums,
+    docs, rows_ref, used_ref, holder_ref, weight_ref, gamma_ref, theta_hbm, high_hbm, low_hbm, gamma_out, out_hbm,
+    terms, theta_ref, high_ref, low_ref, sem, *sums,
 ):
     loads = [
         pltpu.make_async_copy(high_hbm, high_ref, sem.at[0]),
         pltpu.make_async_copy(low_hbm, low_ref, sem.at[1]),
+        pltpu.make_async_copy(theta_hbm, theta_ref, sem.at[3]),
     ]
     for copy in loads:
         copy.start()
@@ -520,7 +527,7 @@
             shape((slots, cols), BF), shape((slots, cols), BF),
         ],
         [VM] * 5 + [AN],
-        [VM] * 6 + [AN] * 2,
+        [VM, AN] + [VM] * 4 + [AN] * 2,
         [
             V((owners, 8, 128), I32),
             V((owners, 8, 128), I32),
@@ -543,7 +550,7 @@
             V((nx, nz, *block), F32),
             V((nz, *block), F32),
             V((nz, *block), F32),
-            D((2,)), D((owners,)), D((owners,)), D((owners,)), D((groups, nz // 2)), D((groups, nz // 2)),
+            D((3,)), D((owners,)), D((owners,)), D((owners,)), D((groups, nz // 2)), D((groups, nz // 2)),
             D((groups, nz // 2)), D((2, groups, nz // 2)),
             D((nz,)), D((nz,)), D((nx, nz)), D((nx, nz)), D((nx, nz)), D((nx, nz)), D((nz,)), D((nz,)),
         ],
@@ -553,11 +560,11 @@
     gamma, stats = call(
         functools.partial(stats_kernel, docs),
         [shape(block), shape((2 * words, 128))],
-        [SM, SM] + [VM] * 4 + [AN] * 2,
+        [SM, SM] + [VM] * 3 + [AN] * 3,
         [VM, AN],
-        [V((2 * slots, 128), F32), V((slots, cols), BF), V((slots, cols), BF), D((3,))]
+        [V((2 * slots, 128), F32), V((owners * docs, cols), F32), V((slots, cols), BF), V((slots, cols), BF), D((4,))]
         + [V((2 * words, 128), F32)] * 4,
-    )(rows.reshape(slots), used, holder, theta, weight, gamma, high, low)
+    )(rows.reshape(slots), used, holder, weight, gamma, theta, high, low)
     return gamma, stats.reshape(words // 8, 2, 8, 128).swapaxes(1, 2).reshape(words, cols)
 
 

time: 148 us -> 137 us (0.926)
  the two profiles are of different devices: /device:TPU:5 before, /device:TPU:2 now
where the time goes in v1:
time: 137 us; the launch traced here: 135 us
  Pallas kernels  134 us (98%)
    pallas_call x1, Pallas kernels, per_device(): call(functools.partial(main_kernel, nx, nz, groups), [shape(block), shape...  116 us
    pallas_call x1, Pallas kernels, per_device(): call(functools.partial(stats_kernel, docs), [shape(block), shape((2 * wor...  18.6 us

profile of v1, /device:TPU:2, one launch (start us, length us, event | category | flops | bytes accessed | tf_op | source)
XLA Modules:
  0.0 135.0 jit_solution(16954439113601851841)
XLA Ops:
  0.6 115.7 %shard_map.77 = (f32[16,256]{1,0:T(8,128)}, f32[512,256]{1,0:T(8,128)}, f32[32,256]{1,0:T(8,128)}, s32[32,256]{1,0:T(8,128)}, s32[64,128]{1,0:T(8,128)}, /*index...) custom-call(s32[16,1,256]{2,1,0:T(1,128)} %bitcast.9, s32[16,256]{1,0:T(8,128)} %row_ref.1, ...), custom_call_target="tpu_custom_call" | custom-call | tf_op jit(solution)/shard_map/pallas_call | solution.py:522
  116.4 18.6 %shard_map.78 = (f32[16,256]{1,0:T(8,128)}, f32[16384,128]{1,0:T(8,128)}) custom-call(s32[8192]{0:T(1024)} %bitcast.8, s32[32,128]{1,0:T(8,128)} %get-tuple-element.13.used_ref, s32[32,256]{1,0:T(8,128)} %get-tuple-element.14.holder_ref, f32[32,256]{1,0:T(8,128)} %get-tuple-element.15.weight_ref, f32[16,256]{1,0:T(8,128)} %get-tuple-element.16.gamma_ref, ...), custom_call_target="tpu_custom_call" | custom-call | tf_op jit(solution)/shard_map/pallas_call | solution.py:560
